TPU v7x, 32 devices: a whole 2x2x4 slice. The times are simulated.
32 devices in a mesh: freq: 2 (over x), param: 4 (over y, core), sens: 4 (over z).
Axes of the slice: x: 2, y: 2, z: 4, core: 2. Of those that a mesh axis runs over, the one named last changes fastest.
Arguments:
- series: bfloat16 [8, 600, 52], P(None, 'sens', 'freq'), may hold values from -6 to 6
- kernel: bfloat16 [2, 32, 600, 4096], P(None, 'freq', 'sens', 'param'), may hold values from -0.1875 to 0.1875
- prior_spectrum: float32 [32], P('freq'), may hold values from 0.3 to 1.5
- prior_scale: float32 [4096], P('param'), may hold values from 0.5 to 2
Outputs:
- adjoint_map: float32 [52, 8, 4096], P('freq', 'sens', 'param')
All inputs are finite; a program needn't handle non-finite values.
Results may differ from a plain program's by a relative error of at most 0.0047.
Values may be sent and summed in bfloat16 or wider, within the bound.
A program may use at most 64 MiB of HBM per device.

v0:
```python
import math
import jax
import jax.numpy as jnp
from jax import lax
from jax.sharding import PartitionSpec as P

LEN = 840
FB_DEV = 16


def extended(cells, sides, width):
    for axis, dim in sides:
        count = lax.axis_size(axis)
        ends = count - 1
        head = lax.slice_in_dim(cells, 0, width, axis=dim)
        tail = lax.slice_in_dim(cells, cells.shape[dim] - width, cells.shape[dim], axis=dim)
        cells = jnp.concatenate(
            [
                lax.ppermute(tail, axis, [(i, (i + 1) % count) for i in range(ends)]),
                cells,
                lax.ppermute(head, axis, [((i + 1) % count, i) for i in range(ends)]),
            ],
            axis=dim,
        )
    return cells


def phase_tables(bin_first, bin_count, time_count):
    bin_index = bin_first + jnp.arange(bin_count, dtype=jnp.int32)
    time_index = jnp.arange(time_count, dtype=jnp.int32)
    product = time_index[:, None] * bin_index[None, :] % LEN
    phase_angle = product.astype(jnp.float32) * (2.0 * math.pi / LEN)
    return (jnp.cos(phase_angle), jnp.sin(phase_angle))


def contract(spectrum, operator):
    return jnp.einsum("bsr,bsp->brp", spectrum, operator, preferred_element_type=jnp.float32)


def local(series, kernel, prior_spectrum, prior_scale):
    highest = lax.Precision.HIGHEST
    groups = lax.axis_size("freq")
    first_bin = lax.axis_index("freq") * FB_DEV
    probes, sens_dev, time_dev = series.shape
    total_times = time_dev * groups
    cosine, sine_part = phase_tables(first_bin, FB_DEV, total_times)
    phase_table = jnp.concatenate([cosine, -sine_part], axis=1)
    series_piece = lax.all_gather(series, "freq", axis=2, tiled=True)
    row_count = series_piece.shape[2]
    flat_rows = series_piece.astype(jnp.float32).reshape(-1, row_count)
    spectra = jnp.dot(flat_rows, phase_table, precision=highest)
    spectra = (spectra * (1.0 / math.sqrt(total_times))).astype(jnp.bfloat16)
    both_parts = (
        spectra.reshape(probes, sens_dev, 2, FB_DEV)
        .transpose(3, 1, 2, 0)
        .reshape(FB_DEV, sens_dev, 2 * probes)
    )
    with_real = contract(both_parts, kernel[0])
    with_imag = contract(both_parts, kernel[1])
    real_part = with_real[:, :probes] + with_imag[:, probes:]
    imag_part = with_real[:, probes:] - with_imag[:, :probes]
    partial_value = jnp.stack([real_part, imag_part])
    summed = lax.psum_scatter(partial_value, "sens", scatter_dimension=2, tiled=True)
    weights = prior_spectrum * (1.0 / math.sqrt(FB_DEV * groups))
    scaled_spec = summed * weights[None, :, None, None]
    arrived = lax.all_to_all(scaled_spec, "freq", split_axis=3, concat_axis=1, tiled=True)
    bin_total = arrived.shape[1]
    item_count = arrived.shape[2]
    col_count = arrived.shape[3]
    cos_all, sin_all = phase_tables(0, bin_total, total_times)
    full_table = jnp.concatenate([cos_all, -sin_all], axis=1)
    flat_rows = arrived.reshape(2 * bin_total, item_count * col_count)
    arranged = jnp.dot(full_table, flat_rows, precision=highest).reshape(
        total_times, item_count, col_count
    )
    image_field = lax.all_to_all(arranged, "freq", split_axis=0, concat_axis=2, tiled=True)
    weighted = image_field * prior_scale
    padded = extended(weighted, (("param", 2),), 1)
    smooth = 0.5 * weighted + 0.25 * (padded[:, :, :-2] + padded[:, :, 2:])
    return smooth * prior_scale


def solution(mesh):
    placed = (P(None, "sens", "freq"), P(None, "freq", "sens", "param"), P("freq"), P("param"))
    return jax.shard_map(
        local, mesh=mesh, in_specs=placed, out_specs=P("freq", "sens", "param"), check_vma=False
    )
```

profile of v0, /device:TPU:1, one launch (start us, length us, event | category | flops | bytes accessed | tf_op | source)
XLA Modules:
  0.0 111.2 jit_solution(6841817095177923095)
XLA Ops:
  6.5 0.1 fusion.32
  6.7 5.6 %all_gather.3 = bf16[8,150,52]{1,0,2:T(8,128)(2,1)S(1)} all-gather(bf16[8,150,26]{1,0,2:T(8,128)(2,1)} %param.4), channel_id=1, replica_groups=mesh['freq'=2,'param'=4,'sens'=4] {'freq'}, dimensions={2}, use_global_device_ids=true | all-gather | bytes 187200 | tf_op jit(solution)/shard_map/all_gather | solution.py:48
  12.3 0.2 reshape.21
  12.5 0.2 fusion.3
  12.8 0.2 reshape.22
  13.0 7.8 %fusion.36 = (bf16[1,16,150,1024]{3,1,2,0:T(8,128)(2,1)S(1)}, bf16[1,16,150,1024]{3,1,2,0:T(8,128)(2,1)}) fusion(bf16[2,16,150,1024]{3,1,2,0:T(8,128)(2,1)} %param.5), kind=kLoop, calls=%fused_computation.55 | loop fusion | bytes 19660800 | tf_op jit(solution)/shard_map/slice | solution.py:58
  20.8 7.8 %fusion = f32[16,16,1024]{2,1,0:T(8,128)S(1)} fusion(bf16[1,16,150,1024]{3,1,2,0:T(8,128)(2,1)} %get-tuple-element.6, bf16[8,150,2,16]{1,0,3,2:T(8,128)(2,1)S(1)} %reshape.22), kind=kOutput, calls=%fused_computation.1 | convolution fusion | flops 78643200 | bytes 6040576 | tf_op jit(solution)/shard_map/bsr,bsp->brp/dot_general | solution.py:37
  28.6 5.6 %fusion.1 = f32[16,16,1024]{2,1,0:T(8,128)S(1)} fusion(bf16[1,16,150,1024]{3,1,2,0:T(8,128)(2,1)S(1)} %get-tuple-element.5, bf16[8,150,2,16]{1,0,3,2:T(8,128)(2,1)S(1)} %reshape.22), kind=kOutput, calls=%fused_computation.3 | convolution fusion | flops 78643200 | bytes 6040576 | tf_op jit(solution)/shard_map/bsr,bsp->brp/dot_general | solution.py:37
  34.2 0.1 fusion.5
  34.3 0.1 pad_maximum_fusion
  34.4 1.6 %copy.43 = f32[2,16,8,1024]{3,1,0,2:T(8,128)} copy(f32[2,16,8,1024]{3,2,1,0:T(8,128)S(1)} %pad_maximum_fusion) | data formatting | bytes 2097152 | tf_op jit(solution)/shard_map/stack | solution.py:62
  36.0 0.0 reduce-scatter.2.cloned.1.call-update
  36.0 29.0 %reduce-scatter.2.cloned.1.call-done = f32[2,16,2,1024]{3,1,0,2:T(8,128)} async-done(((f32[2,16,8,1024]{3,1,0,2:T(8,128)}), f32[2,16,2,1024]{3,1,0,2:T(8,128)}) %reduce-scatter.2.cloned.1.call-update) | async-done | bytes 262160 | tf_op jit(solution)/shard_map/reduce_scatter | solution.py:63
  65.1 1.0 broadcast_multiply_fusion
  66.1 1.3 %copy.44 = f32[2,16,2,1024]{1,2,0,3:T(2,128)S(1)} copy(f32[2,16,2,1024]{3,1,0,2:T(8,128)S(1)} %broadcast_multiply_fusion) | data formatting | bytes 524288 | tf_op jit(solution)/shard_map/mul | solution.py:65
  67.5 3.6 %reshape.26 = f32[2,1,32768]{2,1,0:T(1,128)} reshape(f32[1024,2,2,16]{3,2,1,0:T(2,128)S(1)} %bitcast.53) | data formatting | bytes 524288
  71.0 3.4 %all-to-all-start = ((f32[2,1,32768]{2,1,0:T(1,128)}), f32[2,1,32768]{2,1,0:T(1,128)S(1)}, u32[]{:S(2)}, u32[]{:S(2)}) async-start(f32[2,1,32768]{2,1,0:T(1,128)} %reshape.26), calls=%async_computation.1 | async-start | bytes 524288 | tf_op jit(solution)/shard_map/all_to_all | solution.py:66
  74.5 0.1 sine_negate_fusion
  74.6 3.9 %all-to-all-done = f32[2,1,32768]{2,1,0:T(1,128)S(1)} async-done(((f32[2,1,32768]{2,1,0:T(1,128)}), f32[2,1,32768]{2,1,0:T(1,128)S(1)}, u32[]{:S(2)}, u32[]{:S(2)}) %all-to-all-start) | async-done | bytes 262176 | tf_op jit(solution)/shard_map/all_to_all | solution.py:66
  78.5 0.5 broadcast.17
  79.0 1.4 %reduce = f32[2,32768]{1,0:T(2,128)S(1)} reduce(f32[2,1,32768]{2,1,0:T(1,128)S(1)} %all-to-all-done, f32[]{:T(128)} %broadcast.17), dimensions={1}, to_apply=%all_to_all.24.reduce_sub_computation | reduce | bytes 524292 | tf_op jit(solution)/shard_map/all_to_all | solution.py:66
  80.5 2.8 %reshape.27 = f32[1024,2,2,16]{3,2,1,0:T(2,128)S(1)} reshape(f32[2,32768]{1,0:T(2,128)S(1)} %reduce) | data formatting | bytes 524288
  83.3 1.5 %copy.45 = f32[2,16,2,2,512]{4,2,1,3,0:T(2,128)S(1)} copy(f32[2,16,2,2,512]{1,2,0,4,3:T(2,128)S(1)} %bitcast.54) | data formatting | bytes 524288 | tf_op jit(solution)/shard_map/all_to_all | solution.py:66
  84.7 0.4 fusion.6
  85.1 0.2 copy.47
  85.3 6.1 %all_to_all.33 = f32[52,2,512]{2,1,0:T(2,128)S(1)} all-to-all(f32[52,2,512]{2,1,0:T(2,128)S(1)} %copy.47), channel_id=1, replica_groups=mesh['freq'=2,'param'=4,'sens'=4] {'freq'}, dimensions={0} | all-to-all | bytes 425984 | tf_op jit(solution)/shard_map/all_to_all | solution.py:76
  91.5 0.1 broadcast_multiply_fusion.1
  91.5 0.1 fusion.37
  91.6 6.4 %collective-permute-start = (f32[26,2,1]{2,1,0:T(2,128)S(1)}, f32[26,2,1]{2,1,0:T(2,128)S(1)}, u32[]{:S(2)}, u32[]{:S(2)}) collective-permute-start(f32[26,2,1]{2,1,0:T(2,128)S(1)} %get-tuple-element.9), channel_id=1, source_target_pairs={{0,4},{4,8},{8,12},{1,5},{5,9},{9,13},{2,6},{6,10},{10,14},{3,7},{... | collective-permute-start | bytes 632 | tf_op jit(solution)/shard_map/ppermute | solution.py:19
  98.0 1.9 %collective-permute-start.1 = (f32[26,2,1]{2,1,0:T(2,128)S(1)}, f32[26,2,1]{2,1,0:T(2,128)S(1)}, u32[]{:S(2)}, u32[]{:S(2)}) collective-permute-start(f32[26,2,1]{2,1,0:T(2,128)S(1)} %get-tuple-element.10), channel_id=1, source_target_pairs={{4,0},{8,4},{12,8},{5,1},{9,5},{13,9},{6,2},{10,6},{14,10},{7,3},{... | collective-permute-start | bytes 632 | tf_op jit(solution)/shard_map/ppermute | solution.py:21
  99.9 3.2 %collective-permute-done.1 = f32[26,2,1]{2,1,0:T(2,128)S(1)} collective-permute-done((f32[26,2,1]{2,1,0:T(2,128)S(1)}, f32[26,2,1]{2,1,0:T(2,128)S(1)}, u32[]{:S(2)}, u32[]{:S(2)}) %collective-permute-start.1) | collective-permute-done | bytes 240 | tf_op jit(solution)/shard_map/ppermute | solution.py:21
  103.2 1.2 %fusion.12 = f32[26,2,1024]{2,1,0:T(2,128)} fusion(f32[26,2,1]{2,1,0:T(2,128)S(1)} %collective-permute-done.1, f32[26,2,1024]{2,1,0:T(2,128)S(1)} %broadcast_multiply_fusion.1, f32[26,2,1]{2,1,0:T(2,128)S(1)} %collective-permute-done, f32[1024]{0:T(1024)S(1)} %copy-done), kind=kLoop, calls=%fused_computation.20 | loop fusion | flops 372736 | bytes 430496 | tf_op jit(solution)/shard_map/mul | solution.py:80
  (9 shorter events, 0.0 us)
Async XLA Ops:
  6.5 58.5 %reduce-scatter.2.cloned.1.call-start = ((), (), s32[]{:S(2)}) async-start(), calls=%async_computation.3 | async-start | bytes 1310720 | tf_op jit(solution)/shard_map/reduce_scatter | solution.py:63
  34.2 1.8 %copy-start.1 = (f32[16]{0:T(128)S(1)}, f32[16]{0:T(128)}, u32[]{:S(2)}) copy-start(f32[16]{0:T(128)} %param.6) | copy-start | bytes 196
  67.5 24.0 %copy-start = (f32[1024]{0:T(1024)S(1)}, f32[1024]{0:T(1024)}, u32[]{:S(2)}) copy-start(f32[1024]{0:T(1024)} %param.7) | copy-start | bytes 12292
  71.0 7.5 %all-to-all-start = ((f32[2,1,32768]{2,1,0:T(1,128)}), f32[2,1,32768]{2,1,0:T(1,128)S(1)}, u32[]{:S(2)}, u32[]{:S(2)}) async-start(f32[2,1,32768]{2,1,0:T(1,128)} %reshape.26), calls=%async_computation.1 | async-start | bytes 524288 | tf_op jit(solution)/shard_map/all_to_all | solution.py:66
  91.6 8.3 %collective-permute-start = (f32[26,2,1]{2,1,0:T(2,128)S(1)}, f32[26,2,1]{2,1,0:T(2,128)S(1)}, u32[]{:S(2)}, u32[]{:S(2)}) collective-permute-start(f32[26,2,1]{2,1,0:T(2,128)S(1)} %get-tuple-element.9), channel_id=1, source_target_pairs={{0,4},{4,8},{8,12},{1,5},{5,9},{9,13},{2,6},{6,10},{10,14},{3,7},{... | collective-permute-start | bytes 632 | tf_op jit(solution)/shard_map/ppermute | solution.py:19
  98.0 5.2 %collective-permute-start.1 = (f32[26,2,1]{2,1,0:T(2,128)S(1)}, f32[26,2,1]{2,1,0:T(2,128)S(1)}, u32[]{:S(2)}, u32[]{:S(2)}) collective-permute-start(f32[26,2,1]{2,1,0:T(2,128)S(1)} %get-tuple-element.10), channel_id=1, source_target_pairs={{4,0},{8,4},{12,8},{5,1},{9,5},{13,9},{6,2},{10,6},{14,10},{7,3},{... | collective-permute-start | bytes 632 | tf_op jit(solution)/shard_map/ppermute | solution.py:21
Sparse Core Ops, SparseCore 0:
  36.1 28.8 reduce-scatter.1
where the time goes:
time: 112 us; the launch traced here: 111 us
  waiting for transfers between devices  36.2 us (32%)
  local copies, waits for them, and re-layouts  19.8 us (18%)
  matrix products  14 us (12%)
  between operations  13.6 us (12%)
  starting transfers between devices  11.7 us (10%)
  blocking collectives  11.7 us (10%)
  other arithmetic  4.27 us (4%)
    reduce_scatter x1, waiting for transfers between devices, local(): lax.psum_scatter(partial_value, 'sens', scatter_dimension=2, tiled=True)  29 us
    dot_general x2, matrix products, contract(): jnp.einsum('bsr,bsp->brp', spectrum, operator, preferred_element_type=jnp...  13.4 us
    slice x1, local copies, waits for them, and re-layouts, local(): with_real = contract(both_parts, kernel[0])  7.77 us
    unnamed x6, local copies, waits for them, and re-layouts  6.39 us
    ppermute x1, starting transfers between devices, extended(): lax.ppermute(tail, axis, [(i, (i + 1) % count) for i in range(ends)])  6.36 us
    all_to_all x1, blocking collectives, local(): lax.all_to_all(arranged, 'freq', split_axis=0, concat_axis=2, tiled=True)  6.12 us
    all_gather x1, blocking collectives, local(): series_piece = lax.all_gather(series, 'freq', axis=2, tiled=True)  5.63 us
    all_to_all x1, waiting for transfers between devices, local(): lax.all_to_all(scaled_spec, 'freq', split_axis=3, concat_axis=1, tiled=True)  3.86 us
  transfers between devices with their start and end apart: 4, of which 3 were waited for; matrix products, arithmetic and copies ran while one was open for 0% of the time, Pallas kernels for 0%

commit v1 on v0

--- a/solution.py
+++ b/solution.py
@@ -63,7 +63,12 @@
     summed = lax.psum_scatter(partial_value, "sens", scatter_dimension=2, tiled=True)
     weights = prior_spectrum * (1.0 / math.sqrt(FB_DEV * groups))
     scaled_spec = summed * weights[None, :, None, None]
-    arrived = lax.all_to_all(scaled_spec, "freq", split_axis=3, concat_axis=1, tiled=True)
+    arrived = jnp.concatenate(
+        lax.all_to_all(
+            jnp.stack(jnp.split(scaled_spec, lax.axis_size("freq"), axis=3)), "freq", 0, 0
+        ),
+        axis=1,
+    )
     bin_total = arrived.shape[1]
     item_count = arrived.shape[2]
     col_count = arrived.shape[3]

time: 112 us -> 101 us (0.902)
  local copies, waits for them, and re-layouts: 19.8 us -> 10.3 us
    unnamed x6 -> x4, local copies, waits for them, and re-layouts: 6.39 us -> 0.01 us
    all_to_all x2 -> x0, local copies, waits for them, and re-layouts: 1.96 us -> none  [local(): lax.all_to_all(scaled_spec, 'freq', split_axis=3, concat_axis=1, tiled=True)]
    all_to_all x1 -> x0, other arithmetic: 1.44 us -> none  [local(): lax.all_to_all(scaled_spec, 'freq', split_axis=3, concat_axis=1, tiled=True)]
    mul x1 -> x0, local copies, waits for them, and re-layouts: 1.35 us -> none  [local(): scaled_spec = summed * weights[None, :, None, None]]
where the time goes in v1:
time: 101 us
  waiting for transfers between devices  36.2 us (36%)
  matrix products  14 us (14%)
  between operations  13.5 us (13%)
  starting transfers between devices  11.7 us (12%)
  blocking collectives  11.7 us (12%)
  local copies, waits for them, and re-layouts  10.3 us (10%)
  other arithmetic  3.55 us (4%)
    reduce_scatter x1, waiting for transfers between devices, local(): lax.psum_scatter(partial_value, 'sens', scatter_dimension=2, tiled=True)  29 us
    dot_general x2, matrix products, contract(): jnp.einsum('bsr,bsp->brp', spectrum, operator, preferred_element_type=jnp...  13.4 us
    slice x1, local copies, waits for them, and re-layouts, local(): with_real = contract(both_parts, kernel[0])  7.79 us
    ppermute x1, starting transfers between devices, extended(): lax.ppermute(tail, axis, [(i, (i + 1) % count) for i in range(ends)])  6.35 us
    all_to_all x1, blocking collectives, local(): lax.all_to_all(arranged, 'freq', split_axis=0, concat_axis=2, tiled=True)  6.12 us
    all_gather x1, blocking collectives, local(): series_piece = lax.all_gather(series, 'freq', axis=2, tiled=True)  5.63 us
    all_to_all x1, waiting for transfers between devices, local(): lax.all_to_all(jnp.stack(jnp.split(scaled_spec, lax.axis_size('freq'), ax...  3.86 us
    all_to_all x1, starting transfers between devices, local(): lax.all_to_all(jnp.stack(jnp.split(scaled_spec, lax.axis_size('freq'), ax...  3.44 us
  transfers between devices with their start and end apart: 4, of which 3 were waited for; matrix products, arithmetic and copies ran while one was open for 0% of the time, Pallas kernels for 0%

profile of v1, /device:TPU:1, one launch (start us, length us, event | category | flops | bytes accessed | tf_op | source)
XLA Modules:
  0.0 101.1 jit_solution(10629813969651405531)
XLA Ops:
  6.5 0.0 reduce-scatter.2.cloned.1.call-start
  6.5 0.1 fusion.32
  6.7 5.6 %all_gather.3 = bf16[8,150,52]{1,0,2:T(8,128)(2,1)S(1)} all-gather(bf16[8,150,26]{1,0,2:T(8,128)(2,1)} %param.4), channel_id=1, replica_groups=mesh['freq'=2,'param'=4,'sens'=4] {'freq'}, dimensions={2}, use_global_device_ids=true | all-gather | bytes 187200 | tf_op jit(solution)/shard_map/all_gather | solution.py:48
  12.3 0.2 reshape.20
  12.5 0.2 fusion.3
  12.8 0.2 reshape.21
  13.0 7.8 %fusion.36 = (bf16[1,16,150,1024]{3,1,2,0:T(8,128)(2,1)S(1)}, bf16[1,16,150,1024]{3,1,2,0:T(8,128)(2,1)}) fusion(bf16[2,16,150,1024]{3,1,2,0:T(8,128)(2,1)} %param.5), kind=kLoop, calls=%fused_computation.58 | loop fusion | bytes 19660800 | tf_op jit(solution)/shard_map/slice | solution.py:58
  20.8 7.8 %fusion = f32[16,16,1024]{2,1,0:T(8,128)S(1)} fusion(bf16[1,16,150,1024]{3,1,2,0:T(8,128)(2,1)} %get-tuple-element.6, bf16[8,150,2,16]{1,0,3,2:T(8,128)(2,1)S(1)} %reshape.21), kind=kOutput, calls=%fused_computation.1 | convolution fusion | flops 78643200 | bytes 6040576 | tf_op jit(solution)/shard_map/bsr,bsp->brp/dot_general | solution.py:37
  28.6 5.6 %fusion.1 = f32[16,16,1024]{2,1,0:T(8,128)S(1)} fusion(bf16[1,16,150,1024]{3,1,2,0:T(8,128)(2,1)S(1)} %get-tuple-element.5, bf16[8,150,2,16]{1,0,3,2:T(8,128)(2,1)S(1)} %reshape.21), kind=kOutput, calls=%fused_computation.3 | convolution fusion | flops 78643200 | bytes 6040576 | tf_op jit(solution)/shard_map/bsr,bsp->brp/dot_general | solution.py:37
  34.2 0.1 fusion.5
  34.3 0.0 copy-start
  34.3 0.1 pad_maximum_fusion
  34.4 1.6 %copy.33 = f32[2,16,8,1024]{3,1,0,2:T(8,128)} copy(f32[2,16,8,1024]{3,2,1,0:T(8,128)S(1)} %pad_maximum_fusion) | data formatting | bytes 2097152 | tf_op jit(solution)/shard_map/stack | solution.py:62
  36.0 0.0 reduce-scatter.2.cloned.1.call-update
  36.0 0.0 copy-done.1
  36.1 29.0 %reduce-scatter.2.cloned.1.call-done = f32[2,16,2,1024]{3,1,0,2:T(8,128)} async-done(((f32[2,16,8,1024]{3,1,0,2:T(8,128)}), f32[2,16,2,1024]{3,1,0,2:T(8,128)}) %reduce-scatter.2.cloned.1.call-update) | async-done | bytes 262160 | tf_op jit(solution)/shard_map/reduce_scatter | solution.py:63
  65.1 1.0 %broadcast_multiply_fusion = f32[2,16,2,1024]{3,1,0,2:T(8,128)S(1)} fusion(f32[2,16,2,1024]{3,1,0,2:T(8,128)} %reduce-scatter.2.cloned.1.call-done, f32[16]{0:T(128)S(1)} %broadcast_multiply_fusion.2), kind=kLoop, calls=%fused_computation.26 | loop fusion | flops 65536 | bytes 524352 | tf_op jit(solution)/shard_map/mul | solution.py:65
  66.2 0.7 pad_maximum_fusion.1
  66.9 3.4 %all-to-all-start = ((f32[2,2,16,2,512]{4,2,1,3,0:T(8,128)}), f32[2,2,16,2,512]{4,2,1,3,0:T(8,128)S(1)}, u32[]{:S(2)}, u32[]{:S(2)}) async-start(f32[2,2,16,2,512]{4,2,1,3,0:T(8,128)} %pad_maximum_fusion.1), calls=%async_computation.1 | async-start | bytes 524288 | tf_op jit(solution)/shard_map/all_to_all | solution.py:67
  70.3 0.1 sine_negate_fusion
  70.5 3.9 %all-to-all-done = f32[2,2,16,2,512]{4,2,1,3,0:T(8,128)S(1)} async-done(((f32[2,2,16,2,512]{4,2,1,3,0:T(8,128)}), f32[2,2,16,2,512]{4,2,1,3,0:T(8,128)S(1)}, u32[]{:S(2)}, u32[]{:S(2)}) %all-to-all-start) | async-done | bytes 262176 | tf_op jit(solution)/shard_map/all_to_all | solution.py:67
  74.3 0.2 copy.34
  74.6 0.4 fusion.6
  75.0 0.2 copy.36
  75.1 6.1 %all_to_all.23 = f32[52,2,512]{2,1,0:T(2,128)S(1)} all-to-all(f32[52,2,512]{2,1,0:T(2,128)S(1)} %copy.36), channel_id=1, replica_groups=mesh['freq'=2,'param'=4,'sens'=4] {'freq'}, dimensions={0} | all-to-all | bytes 425984 | tf_op jit(solution)/shard_map/all_to_all | solution.py:81
  81.3 0.1 broadcast_multiply_fusion.1
  81.4 0.1 fusion.37
  81.5 6.4 %collective-permute-start = (f32[26,2,1]{2,1,0:T(2,128)S(1)}, f32[26,2,1]{2,1,0:T(2,128)S(1)}, u32[]{:S(2)}, u32[]{:S(2)}) collective-permute-start(f32[26,2,1]{2,1,0:T(2,128)S(1)} %get-tuple-element.11), channel_id=1, source_target_pairs={{0,4},{4,8},{8,12},{1,5},{5,9},{9,13},{2,6},{6,10},{10,14},{3,7},{... | collective-permute-start | bytes 632 | tf_op jit(solution)/shard_map/ppermute | solution.py:19
  87.8 1.9 %collective-permute-start.1 = (f32[26,2,1]{2,1,0:T(2,128)S(1)}, f32[26,2,1]{2,1,0:T(2,128)S(1)}, u32[]{:S(2)}, u32[]{:S(2)}) collective-permute-start(f32[26,2,1]{2,1,0:T(2,128)S(1)} %get-tuple-element.12), channel_id=1, source_target_pairs={{4,0},{8,4},{12,8},{5,1},{9,5},{13,9},{6,2},{10,6},{14,10},{7,3},{... | collective-permute-start | bytes 632 | tf_op jit(solution)/shard_map/ppermute | solution.py:21
  89.7 0.0 collective-permute-done
  89.8 3.2 %collective-permute-done.1 = f32[26,2,1]{2,1,0:T(2,128)S(1)} collective-permute-done((f32[26,2,1]{2,1,0:T(2,128)S(1)}, f32[26,2,1]{2,1,0:T(2,128)S(1)}, u32[]{:S(2)}, u32[]{:S(2)}) %collective-permute-start.1) | collective-permute-done | bytes 240 | tf_op jit(solution)/shard_map/ppermute | solution.py:21
  93.0 1.2 %fusion.12 = f32[26,2,1024]{2,1,0:T(2,128)} fusion(f32[26,2,1]{2,1,0:T(2,128)S(1)} %collective-permute-done.1, f32[26,2,1024]{2,1,0:T(2,128)S(1)} %broadcast_multiply_fusion.1, f32[26,2,1]{2,1,0:T(2,128)S(1)} %collective-permute-done, f32[1024]{0:T(1024)S(1)} %copy-done), kind=kLoop, calls=%fused_computation.21 | loop fusion | flops 372736 | bytes 430496 | tf_op jit(solution)/shard_map/mul | solution.py:85
  (6 shorter events, 0.0 us)
Async XLA Ops:
  6.5 58.6 %reduce-scatter.2.cloned.1.call-start = ((), (), s32[]{:S(2)}) async-start(), calls=%async_computation.3 | async-start | bytes 1310720 | tf_op jit(solution)/shard_map/reduce_scatter | solution.py:63
  34.2 1.9 %copy-start.1 = (f32[16]{0:T(128)S(1)}, f32[16]{0:T(128)}, u32[]{:S(2)}) copy-start(f32[16]{0:T(128)} %param.6) | copy-start | bytes 196
  34.3 46.9 %copy-start = (f32[1024]{0:T(1024)S(1)}, f32[1024]{0:T(1024)}, u32[]{:S(2)}) copy-start(f32[1024]{0:T(1024)} %param.7) | copy-start | bytes 12292
  66.9 7.5 %all-to-all-start = ((f32[2,2,16,2,512]{4,2,1,3,0:T(8,128)}), f32[2,2,16,2,512]{4,2,1,3,0:T(8,128)S(1)}, u32[]{:S(2)}, u32[]{:S(2)}) async-start(f32[2,2,16,2,512]{4,2,1,3,0:T(8,128)} %pad_maximum_fusion.1), calls=%async_computation.1 | async-start | bytes 524288 | tf_op jit(solution)/shard_map/all_to_all | solution.py:67
  81.5 8.3 %collective-permute-start = (f32[26,2,1]{2,1,0:T(2,128)S(1)}, f32[26,2,1]{2,1,0:T(2,128)S(1)}, u32[]{:S(2)}, u32[]{:S(2)}) collective-permute-start(f32[26,2,1]{2,1,0:T(2,128)S(1)} %get-tuple-element.11), channel_id=1, source_target_pairs={{0,4},{4,8},{8,12},{1,5},{5,9},{9,13},{2,6},{6,10},{10,14},{3,7},{... | collective-permute-start | bytes 632 | tf_op jit(solution)/shard_map/ppermute | solution.py:19
  87.8 5.2 %collective-permute-start.1 = (f32[26,2,1]{2,1,0:T(2,128)S(1)}, f32[26,2,1]{2,1,0:T(2,128)S(1)}, u32[]{:S(2)}, u32[]{:S(2)}) collective-permute-start(f32[26,2,1]{2,1,0:T(2,128)S(1)} %get-tuple-element.12), channel_id=1, source_target_pairs={{4,0},{8,4},{12,8},{5,1},{9,5},{13,9},{6,2},{10,6},{14,10},{7,3},{... | collective-permute-start | bytes 632 | tf_op jit(solution)/shard_map/ppermute | solution.py:21
Sparse Core Ops, SparseCore 0:
  36.2 28.8 reduce-scatter.1
